TPU v7x, 32 devices: a whole 2x2x4 slice. The times are simulated.
32 devices in a mesh: row: 4 (over z), col: 4 (over x, core), depth: 2 (over y).
Axes of the slice: x: 2, y: 2, z: 4, core: 2. Of those that a mesh axis runs over, the one named last changes fastest.
Arguments:
- heads_concat: bfloat16 [2048, 16384], P('row', ('depth', 'col')), may hold values from -6 to 6
- w_out: bfloat16 [16384, 7168], P(('depth', 'row'), 'col'), may hold values from -0.046875 to 0.046875
Outputs:
- projected: bfloat16 [2048, 7168], P('row', ('col', 'depth'))
All inputs are finite; a program needn't handle non-finite values.
Results may differ from a plain program's by a relative error of at most 0.001.
Values may be sent and summed in bfloat16 or wider, within the bound.
A program may use at most 128 MiB of HBM per device.

v0:
```python
import jax
import jax.numpy as jnp
from jax import lax
from jax.sharding import PartitionSpec as P


def per_device(heads_concat, w_out):
    head_half = lax.all_gather(heads_concat, "col", axis=1, tiled=True)
    weight_half = lax.all_gather(w_out, "row", axis=0, tiled=True)
    partial_sum = jnp.dot(head_half, weight_half, preferred_element_type=jnp.float32)
    summed = lax.psum_scatter(partial_sum, "depth", scatter_dimension=1, tiled=True)
    return summed.astype(jnp.bfloat16)


def solution(mesh):
    return jax.shard_map(
        per_device,
        mesh=mesh,
        in_specs=(P("row", ("depth", "col")), P(("depth", "row"), "col")),
        out_specs=P("row", ("col", "depth")),
        check_vma=False,
    )
```

profile of v0, /device:TPU:11, one launch (start us, length us, event | category | flops | bytes accessed | tf_op | source)
XLA Modules:
  0.0 642.1 jit_solution(13111015978111093550)
XLA Ops:
  6.5 0.0 all-gather.3.cloned.1.call-start
  6.5 0.7 all-gather.3.cloned.1.call-update
  7.3 0.0 all-gather.5.cloned.1.call-start
  7.3 0.7 all-gather.5.cloned.1.call-update
  8.0 0.0 reduce-scatter.2.cloned.1.call-start
  8.1 59.8 %all-gather.3.cloned.1.call-done = bf16[512,8192]{1,0:T(8,128)(2,1)} async-done(((bf16[512,2048]{1,0:T(8,128)(2,1)}), bf16[512,8192]{1,0:T(8,128)(2,1)}) %all-gather.3.cloned.1.call-update) | async-done | bytes 8388624 | tf_op jit(solution)/shard_map/all_gather | solution.py:8
  67.8 492.3 %all-gather.5.cloned.1.call-done = bf16[8192,1792]{1,0:T(8,128)(2,1)} async-done(((bf16[2048,1792]{1,0:T(8,128)(2,1)}), bf16[8192,1792]{1,0:T(8,128)(2,1)}) %all-gather.5.cloned.1.call-update) | async-done | bytes 29360144 | tf_op jit(solution)/shard_map/all_gather | solution.py:9
  560.1 22.7 %fusion = f32[512,1792]{1,0:T(8,128)} fusion(bf16[512,8192]{1,0:T(8,128)(2,1)} %all-gather.3.cloned.1.call-done, bf16[8192,1792]{1,0:T(8,128)(2,1)} %all-gather.5.cloned.1.call-done), kind=kOutput, calls=%fused_computation | convolution fusion | flops 15032385536 | bytes 41418752 | tf_op jit(solution)/shard_map/dot_general | solution.py:10
  582.8 0.0 reduce-scatter.2.cloned.1.call-update
  582.8 50.3 %reduce-scatter.2.cloned.1.call-done = f32[512,896]{1,0:T(8,128)} async-done(((f32[512,1792]{1,0:T(8,128)}), f32[512,896]{1,0:T(8,128)}) %reduce-scatter.2.cloned.1.call-update) | async-done | bytes 1835024 | tf_op jit(solution)/shard_map/reduce_scatter | solution.py:11
  633.1 2.5 convert_element_type.3
Async XLA Ops:
  6.5 61.3 %all-gather.3.cloned.1.call-start = ((), (), s32[]{:S(2)}) async-start(), calls=%async_computation.1 | async-start | bytes 10485760 | tf_op jit(solution)/shard_map/all_gather | solution.py:8
  7.3 552.9 %all-gather.5.cloned.1.call-start = ((), (), s32[]{:S(2)}) async-start(), calls=%async_computation.2 | async-start | bytes 36700160 | tf_op jit(solution)/shard_map/all_gather | solution.py:9
  8.0 625.1 %reduce-scatter.2.cloned.1.call-start = ((), (), s32[]{:S(2)}) async-start(), calls=%async_computation.3 | async-start | bytes 5505024 | tf_op jit(solution)/shard_map/reduce_scatter | solution.py:11
Sparse Core Ops, SparseCore 0:
  8.9 58.8 all-gather.2
  69.4 490.6 all-gather.4
  582.9 50.1 reduce-scatter.1
where the time goes:
time: 644 us; the launch traced here: 642 us
  waiting for transfers between devices  604 us (94%)
  matrix products  22.7 us (4%)
  between operations  13.1 us (2%)
    all_gather x1, waiting for transfers between devices, per_device(): weight_half = lax.all_gather(w_out, 'row', axis=0, tiled=True)  492 us
    all_gather x1, waiting for transfers between devices, per_device(): head_half = lax.all_gather(heads_concat, 'col', axis=1, tiled=True)  59.8 us
    reduce_scatter x1, waiting for transfers between devices, per_device(): lax.psum_scatter(partial_sum, 'depth', scatter_dimension=1, tiled=True)  50.3 us
    dot_general x1, matrix products, per_device(): jnp.dot(head_half, weight_half, preferred_element_type=jnp.float32)  22.7 us
  transfers between devices with their start and end apart: 3, of which 3 were waited for; matrix products, arithmetic and copies ran while one was open for 0% of the time, Pallas kernels for 0%

commit v1 on v0

v1 whole, which is shorter than its diff:
```python
import functools

import jax
import jax.numpy as jnp
from jax import lax
from jax.experimental import pallas as pl
from jax.experimental.pallas import tpu as pltpu
from jax.sharding import PartitionSpec as P

MESH = pl.DeviceIdType.MESH
CORES = 2
LAG = 4
VMEM_BYTES = 66_000_000


def kernel(rows, cols, aligned, a_ref, w_ref, o_ref, w, a, own, out_y, in_y, chain,
           w_sem, s1_send, s1_recv, x_send, x_recv, c_send, c_recv, f_send, f_recv,
           y_send, y_recv, z_send, z_recv):
    r, j, d = lax.axis_index("row"), lax.axis_index("col"), lax.axis_index("depth")
    chips = cols // CORES
    x, core = j // CORES, j % CORES
    share = rows // cols
    tq, kb = a.shape[2], a.shape[3]
    nh = own.shape[3]
    steps = rows * cols
    mate = {"row": r, "col": x * CORES + 1 - core, "depth": d}
    across = {"row": r, "col": j, "depth": 1 - d}
    below = {"row": lax.rem(r + rows - 1, rows), "col": j, "depth": d}
    above = {"row": lax.rem(r + 1, rows), "col": j, "depth": d}
    source_col = r // share

    def x_col(dx):
        return lax.rem(x + dx, chips) * CORES + core

    def x_peer(dx):
        return {"row": r, "col": x_col(dx), "depth": d}

    w_copy = pltpu.make_async_copy(w_ref, w, w_sem)
    w_copy.start()

    barrier = pltpu.get_barrier_semaphore()

    def greet(device):
        pl.semaphore_signal(barrier, inc=1, device_id=device, device_id_type=MESH)

    for t in range(rows):
        pl.when(jnp.logical_or(r != t, source_col != j))(
            lambda t=t: greet({"row": t, "col": source_col, "depth": d})
        )
    for dx in range(1, chips):
        greet(x_peer(dx))
    greet(mate)
    greet(across)
    pl.when(r > 0)(lambda: greet(below))
    pl.when(r < rows - 1)(lambda: greet(above))
    pl.semaphore_wait(
        barrier,
        share * cols + chips
        + jnp.where(source_col != j, 1, 0)
        + jnp.where(r > 0, 1, 0)
        + jnp.where(r < rows - 1, 1, 0),
    )

    def remote(src, dst, send, recv, device):
        return pltpu.make_async_remote_copy(
            src_ref=src, dst_ref=dst, send_sem=send, recv_sem=recv,
            device_id=device, device_id_type=MESH,
        )

    def first(i, q):
        target = {"row": j * share + i, "col": q, "depth": d}
        source = a_ref.at[pl.ds(q * tq, tq), pl.ds(i * kb, kb)]
        return remote(source, a.at[r, q], s1_send.at[i, q], s1_recv.at[r], target)

    def is_me(i, q):
        return jnp.logical_and(r == j * share + i, j == q)

    for i in range(share):
        for q in range(cols):
            @pl.when(is_me(i, q))
            def _():
                pltpu.make_async_copy(
                    a_ref.at[pl.ds(q * tq, tq), pl.ds(i * kb, kb)],
                    a.at[r, q], s1_recv.at[r],
                ).start()

            @pl.when(jnp.logical_not(is_me(i, q)))
            def _():
                first(i, q).start()

    def to_x(t, dx):
        return remote(a.at[t, j], a.at[t, j], x_send.at[dx - 1, t], x_recv.at[dx - 1, t], x_peer(dx))

    def to_mate(t):
        return remote(a.at[t, j], a.at[t, j], c_send.at[t], c_recv.at[t], mate)

    def forward(t, dx):
        col = x_col(chips - dx)
        return remote(a.at[t, col], a.at[t, col], f_send.at[dx - 1, t], f_recv.at[dx - 1, t], mate)

    def arrived(slot, sem):
        pltpu.make_async_copy(slot, slot, sem).wait()

    def spread(t):
        arrived(a.at[t, j], s1_recv.at[t])
        for dx in range(1, chips):
            to_x(t, dx).start()
        to_mate(t).start()

    def relay(t):
        for dx in range(1, chips):
            arrived(a.at[t, x_col(chips - dx)], x_recv.at[dx - 1, t])
            forward(t, dx).start()

    def complete(t):
        arrived(a.at[t, x * CORES + 1 - core], c_recv.at[t])
        for dx in range(1, chips):
            col = lax.rem(x + chips - dx, chips) * CORES + 1 - core
            arrived(a.at[t, col], f_recv.at[dx - 1, t])

    def half(h):
        if aligned:
            return w[:, pl.ds(pl.multiple_of(h * nh, 128), nh)]
        return w[h]

    def y_copy(t, q):
        return remote(out_y.at[t, q], in_y.at[t, q], y_send.at[t, q], y_recv.at[t, q], across)

    def down(t, q):
        return remote(own.at[t, q], chain.at[t, q], z_send.at[t, q], z_recv.at[t, q], below)

    def up(t, q):
        return remote(own.at[t, q], chain.at[t + 1, q], z_send.at[t, q], z_recv.at[t + 1, q], above)

    def place(s):
        pair, q = s // (2 * cols), s % (2 * cols) // 2
        return jnp.where(s % 2 == 0, pair, rows - 1 - pair), q

    def multiply(s):
        t, q = place(s)
        block = a[t, q]
        out_y[t, q] = jnp.dot(block, half(1 - d), preferred_element_type=jnp.float32)
        own[t, q] = jnp.dot(block, half(d), preferred_element_type=jnp.float32)
        y_copy(t, q).start()

    def finish(s):
        t, q = place(s)
        arrived(in_y.at[t, q], y_recv.at[t, q])
        own[t, q] += in_y[t, q]

        @pl.when(jnp.logical_and(t <= r, r < rows - 1))
        def _():
            arrived(chain.at[t, q], z_recv.at[t, q])
            own[t, q] += chain[t, q]

        @pl.when(jnp.logical_and(t >= r, r > 0))
        def _():
            arrived(chain.at[t + 1, q], z_recv.at[t + 1, q])
            own[t, q] += chain[t + 1, q]

        pl.when(t < r)(lambda: down(t, q).start())
        pl.when(t > r)(lambda: up(t, q).start())

        @pl.when(t == r)
        def _():
            o_ref[pl.ds(pl.multiple_of(q * tq, tq), tq), :] = own[t, q].astype(o_ref.dtype)

    spread(0)
    spread(rows - 1)
    relay(0)
    relay(rows - 1)
    w_copy.wait()

    def step(s, carry):
        pair, at = s // (2 * cols), s % (2 * cols)

        @pl.when(at == 0)
        def _():
            complete(pair)
            complete(rows - 1 - pair)

        @pl.when(s < steps)
        def _():
            multiply(s)

        more = pair + 1 < rows // 2

        @pl.when(jnp.logical_and(more, at == 1))
        def _():
            spread(pair + 1)
            spread(rows - 2 - pair)

        @pl.when(jnp.logical_and(more, at == 4))
        def _():
            relay(pair + 1)
            relay(rows - 2 - pair)

        @pl.when(s >= LAG)
        def _():
            finish(s - LAG)

        return carry

    lax.fori_loop(0, steps, step, 0)

    def last(s, carry):
        finish(s)
        return carry

    lax.fori_loop(steps - LAG, steps, last, 0)

    for i in range(share):
        for q in range(cols):
            pl.when(jnp.logical_not(is_me(i, q)))(lambda i=i, q=q: first(i, q).wait_send())

    def drain(t, carry):
        for dx in range(1, chips):
            to_x(t, dx).wait_send()
            forward(t, dx).wait_send()
        to_mate(t).wait_send()
        for q in range(cols):
            y_copy(t, q).wait_send()
            pl.when(t != r)(lambda q=q: down(t, q).wait_send())
        return carry

    lax.fori_loop(0, rows, drain, 0)


def project(rows, cols, heads, w_out):
    tokens = heads.shape[0]
    kb, n = w_out.shape
    nh, tq = n // 2, tokens // cols
    chips = cols // CORES
    aligned = nh % 128 == 0
    w_shape = (kb, n)
    if not aligned:
        w_out = jnp.stack([w_out[:, :nh], w_out[:, nh:]])
        w_shape = (2, kb, nh)
    dma = pltpu.SemaphoreType.DMA
    f32 = jnp.float32
    return pl.pallas_call(
        functools.partial(kernel, rows, cols, aligned),
        out_shape=jax.ShapeDtypeStruct((tokens, nh), jnp.bfloat16),
        in_specs=[pl.BlockSpec(memory_space=pltpu.HBM)] * 2,
        out_specs=pl.BlockSpec(memory_space=pltpu.VMEM),
        scratch_shapes=[
            pltpu.VMEM(w_shape, jnp.bfloat16),
            pltpu.VMEM((rows, cols, tq, kb), jnp.bfloat16),
            pltpu.VMEM((rows, cols, tq, nh), f32),
            pltpu.VMEM((rows, cols, tq, nh), f32),
            pltpu.VMEM((rows, cols, tq, nh), f32),
            pltpu.VMEM((rows + 1, cols, tq, nh), f32),
            dma,
            dma((rows // cols, cols)), dma((rows,)),
            dma((chips - 1, rows)), dma((chips - 1, rows)),
            dma((rows,)), dma((rows,)),
            dma((chips - 1, rows)), dma((chips - 1, rows)),
            dma((rows, cols)), dma((rows, cols)),
            dma((rows, cols)), dma((rows + 1, cols)),
        ],
        compiler_params=pltpu.CompilerParams(
            collective_id=0, has_side_effects=True, vmem_limit_bytes=VMEM_BYTES
        ),
    )(heads, w_out)


def solution(mesh):
    rows, cols = mesh.shape["row"], mesh.shape["col"]

    def per_device(heads, w_out):
        tokens, n = heads.shape[0], w_out.shape[1]
        lanes = -(-n // 256) * 128
        slots = 17 * rows * tokens * lanes
        calls = 1
        while slots // calls > VMEM_BYTES // 2:
            calls *= 2
        size = tokens // calls
        parts = [
            project(rows, cols, heads[c * size:(c + 1) * size], w_out)
            for c in range(calls)
        ]
        return parts[0] if calls == 1 else jnp.concatenate(parts, axis=0)

    return jax.shard_map(
        per_device,
        mesh=mesh,
        in_specs=(P("row", ("depth", "col")), P(("depth", "row"), "col")),
        out_specs=P("row", ("col", "depth")),
        check_vma=False,
    )
```

time: 644 us -> 428 us (0.66)
  the two profiles are of different devices: /device:TPU:11 before, /device:TPU:20 now
where the time goes in v1:
time: 428 us
  Pallas kernels  425 us (99%)
    pallas_call x1, Pallas kernels, project(): pl.pallas_call(functools.partial(kernel, rows, cols, aligned), out_shape=...  425 us

profile of v1, /device:TPU:20, one launch (start us, length us, event | category | flops | bytes accessed | tf_op | source)
XLA Modules:
  0.0 427.7 jit_solution(2078331596467981244)
XLA Ops:
  0.0 425.5 %shard_map.28 = bf16[512,896]{1,0:T(8,128)(2,1)} custom-call(bf16[512,2048]{1,0:T(8,128)(2,1)} %a_ref.1, bf16[2048,1792]{1,0:T(8,128)(2,1)} %w_ref.1), custom_call_target="tpu_custom_call" | custom-call | tf_op jit(solution)/shard_map/pallas_call | solution.py:241
  425.5 2.2 copy.4

commit v2 on v1

--- a/solution.py
+++ b/solution.py
@@ -9,8 +9,14 @@
 
 MESH = pl.DeviceIdType.MESH
 CORES = 2
-LAG = 4
+LAG = 2
 VMEM_BYTES = 66_000_000
+
+
+def finishing(rows, r):
+    downward = [(2 * t + rows - 1 - r, t) for t in range(r)]
+    upward = [(2 * (rows - 1 - t) + r, t) for t in range(r + 1, rows)]
+    return [t for _, t in sorted(downward + upward)] + [r]
 
 
 def kernel(rows, cols, aligned, a_ref, w_ref, o_ref, w, a, own, out_y, in_y, chain,
@@ -112,12 +118,6 @@
             arrived(a.at[t, x_col(chips - dx)], x_recv.at[dx - 1, t])
             forward(t, dx).start()
 
-    def complete(t):
-        arrived(a.at[t, x * CORES + 1 - core], c_recv.at[t])
-        for dx in range(1, chips):
-            col = lax.rem(x + chips - dx, chips) * CORES + 1 - core
-            arrived(a.at[t, col], f_recv.at[dx - 1, t])
-
     def half(h):
         if aligned:
             return w[:, pl.ds(pl.multiple_of(h * nh, 128), nh)]
@@ -132,19 +132,31 @@
     def up(t, q):
         return remote(own.at[t, q], chain.at[t + 1, q], z_send.at[t, q], z_recv.at[t + 1, q], above)
 
-    def place(s):
-        pair, q = s // (2 * cols), s % (2 * cols) // 2
-        return jnp.where(s % 2 == 0, pair, rows - 1 - pair), q
-
-    def multiply(s):
-        t, q = place(s)
+    order = []
+    for p in range(rows):
+        block = jnp.int32(0)
+        for row in range(rows):
+            block = jnp.where(r == row, finishing(rows, row)[p], block)
+        order.append(block)
+
+    def pick(p):
+        block = order[0]
+        for n in range(1, rows):
+            block = jnp.where(p == n, order[n], block)
+        return block
+
+    def column(k):
+        chip = lax.rem(x + chips - k // CORES, chips)
+        return chip * CORES + jnp.where(k % CORES == 0, core, 1 - core)
+
+    def multiply(t, q):
         block = a[t, q]
         out_y[t, q] = jnp.dot(block, half(1 - d), preferred_element_type=jnp.float32)
         own[t, q] = jnp.dot(block, half(d), preferred_element_type=jnp.float32)
         y_copy(t, q).start()
 
     def finish(s):
-        t, q = place(s)
+        t, q = pick(s // cols), column(s % cols)
         arrived(in_y.at[t, q], y_recv.at[t, q])
         own[t, q] += in_y[t, q]
 
@@ -165,40 +177,31 @@
         def _():
             o_ref[pl.ds(pl.multiple_of(q * tq, tq), tq), :] = own[t, q].astype(o_ref.dtype)
 
-    spread(0)
-    spread(rows - 1)
-    relay(0)
-    relay(rows - 1)
+    spread(r)
     w_copy.wait()
 
     def step(s, carry):
-        pair, at = s // (2 * cols), s % (2 * cols)
-
-        @pl.when(at == 0)
-        def _():
-            complete(pair)
-            complete(rows - 1 - pair)
-
-        @pl.when(s < steps)
-        def _():
-            multiply(s)
-
-        more = pair + 1 < rows // 2
-
-        @pl.when(jnp.logical_and(more, at == 1))
-        def _():
-            spread(pair + 1)
-            spread(rows - 2 - pair)
-
-        @pl.when(jnp.logical_and(more, at == 4))
-        def _():
-            relay(pair + 1)
-            relay(rows - 2 - pair)
-
-        @pl.when(s >= LAG)
-        def _():
-            finish(s - LAG)
-
+        p, k = s // cols, s % cols
+        t = pick(lax.rem(p + rows - 1, rows))
+
+        @pl.when(k == 1)
+        def _():
+            arrived(a.at[t, column(1)], c_recv.at[t])
+
+        pl.when(k == CORES)(lambda: relay(t))
+        for dx in range(1, chips):
+            @pl.when(k == CORES * dx + 1)
+            def _():
+                arrived(a.at[t, column(CORES * dx + 1)], f_recv.at[dx - 1, t])
+
+        multiply(t, column(k))
+
+        @pl.when(s == cols - 1)
+        def _():
+            for n in range(rows - 1):
+                spread(order[n])
+
+        pl.when(s >= cols + LAG)(lambda: finish(s - cols - LAG))
         return carry
 
     lax.fori_loop(0, steps, step, 0)
@@ -207,7 +210,7 @@
         finish(s)
         return carry
 
-    lax.fori_loop(steps - LAG, steps, last, 0)
+    lax.fori_loop(steps - cols - LAG, steps, last, 0)
 
     for i in range(share):
         for q in range(cols):

time: 428 us -> 222 us (0.52)
  the two profiles are of different devices: /device:TPU:20 before, /device:TPU:11 now
where the time goes in v2:
time: 222 us
  Pallas kernels  220 us (99%)
    pallas_call x1, Pallas kernels, project(): pl.pallas_call(functools.partial(kernel, rows, cols, aligned), out_shape=...  220 us

profile of v2, /device:TPU:11, one launch (start us, length us, event | category | flops | bytes accessed | tf_op | source)
XLA Modules:
  0.0 222.2 jit_solution(10650927260466018435)
XLA Ops:
  0.0 220.0 %shard_map.28 = bf16[512,896]{1,0:T(8,128)(2,1)} custom-call(bf16[512,2048]{1,0:T(8,128)(2,1)} %a_ref.1, bf16[2048,1792]{1,0:T(8,128)(2,1)} %w_ref.1), custom_call_target="tpu_custom_call" | custom-call | tf_op jit(solution)/shard_map/pallas_call | solution.py:244
  220.0 2.2 copy.4

commit v3 on v2

--- a/solution.py
+++ b/solution.py
@@ -145,6 +145,10 @@
             block = jnp.where(p == n, order[n], block)
         return block
 
+    def place(n):
+        k = n // (CORES * (rows - 1)) * CORES + n % CORES
+        return n // CORES % (rows - 1), k
+
     def column(k):
         chip = lax.rem(x + chips - k // CORES, chips)
         return chip * CORES + jnp.where(k % CORES == 0, core, 1 - core)
@@ -156,7 +160,10 @@
         y_copy(t, q).start()
 
     def finish(s):
-        t, q = pick(s // cols), column(s % cols)
+        p, k = place(s)
+        mine = s >= steps - cols
+        t = jnp.where(mine, r, pick(p))
+        q = column(jnp.where(mine, s - (steps - cols), k))
         arrived(in_y.at[t, q], y_recv.at[t, q])
         own[t, q] += in_y[t, q]
 
@@ -177,12 +184,15 @@
         def _():
             o_ref[pl.ds(pl.multiple_of(q * tq, tq), tq), :] = own[t, q].astype(o_ref.dtype)
 
-    spread(r)
     w_copy.wait()
 
     def step(s, carry):
-        p, k = s // cols, s % cols
-        t = pick(lax.rem(p + rows - 1, rows))
+        p, k = place(s - cols)
+        mine = s < cols
+        t = jnp.where(mine, r, pick(p))
+        k = jnp.where(mine, s, k)
+
+        pl.when(k == 0)(lambda: spread(t))
 
         @pl.when(k == 1)
         def _():
@@ -195,11 +205,6 @@
                 arrived(a.at[t, column(CORES * dx + 1)], f_recv.at[dx - 1, t])
 
         multiply(t, column(k))
-
-        @pl.when(s == cols - 1)
-        def _():
-            for n in range(rows - 1):
-                spread(order[n])
 
         pl.when(s >= cols + LAG)(lambda: finish(s - cols - LAG))
         return carry

time: 222 us -> 216 us (0.973)
  Pallas kernels: 220 us -> 213 us
    pallas_call x1, Pallas kernels: 220 us -> 213 us  [project(): pl.pallas_call(functools.partial(kernel, rows, cols, aligned), out_shape=...]
where the time goes in v3:
time: 216 us; the launch traced here: 215 us
  Pallas kernels  213 us (99%)
  local copies, waits for them, and re-layouts  2.18 us (1%)
    pallas_call x1, Pallas kernels, project(): pl.pallas_call(functools.partial(kernel, rows, cols, aligned), out_shape=...  213 us

profile of v3, /device:TPU:11, one launch (start us, length us, event | category | flops | bytes accessed | tf_op | source)
XLA Modules:
  0.0 214.8 jit_solution(12640694512669598213)
XLA Ops:
  0.0 212.6 %shard_map.28 = bf16[512,896]{1,0:T(8,128)(2,1)} custom-call(bf16[512,2048]{1,0:T(8,128)(2,1)} %a_ref.1, bf16[2048,1792]{1,0:T(8,128)(2,1)} %w_ref.1), custom_call_target="tpu_custom_call" | custom-call | tf_op jit(solution)/shard_map/pallas_call | solution.py:249
  212.6 2.2 %copy.4 = bf16[512,896]{1,0:T(8,128)(2,1)} copy(bf16[512,896]{1,0:T(8,128)(2,1)} %shard_map.28) | data formatting | bytes 1835008
